TPU v7x, 256 devices: a whole 4x4x8 slice. The times are simulated.
256 devices in a mesh: row: 8 (over y, core), col: 32 (over x, z).
Axes of the slice: x: 4, y: 4, z: 8, core: 2. Of those that a mesh axis runs over, the one named last changes fastest.
Arguments:
- x_blocks: bfloat16 [8, 32, 42, 128, 128], P('row', 'col'), may hold values from -1.1953125 to 1.1953125
- x_slots: int32 [8, 32, 42], replicated, may hold values from 0 to 255, as said below
- x_count: int32 [8, 32], replicated, may hold values from 21 to 42, as said below
- s_slots: int32 [8, 32, 2], replicated, may hold values from 0 to 15, as said below
- s_count: int32 [8, 32], replicated, may hold values from 1 to 2, as said below
Outputs:
- square_blocks: bfloat16 [8, 32, 2, 128, 128], P('row', 'col')
- result_blocks: bfloat16 [8, 32, 2, 128, 128], P('row', 'col')
Inputs may be any that keep to these rules, and one draw needn't show every extreme that they name: `x_slots`: in each tile the live slots hold distinct positions; the live blocks whose position % 32 is below 2 come first among the live slots, at most 2 of them, and some tile has exactly 2. Positions of slots that are not live are arbitrary within the range. `x_count`: some tile has exactly 42 live slots. `s_slots`: in each tile the live slots hold distinct positions. `s_count`: some tile has exactly 2 live slots.
All inputs are finite; a program needn't handle non-finite values.
Results may differ from a plain program's by a relative error of at most 0.0049.
Values may be sent and summed in bfloat16 or wider, within the bound.
A program may use at most 128 MiB of HBM per device.

v0:
```python
import math
import jax
import jax.numpy as jnp
from jax import lax
from jax.sharding import PartitionSpec as P

RB = 8
JW = 2
CAPW = 2


def laid_out(pieces, dim):
    dims = list(pieces.shape[1:])
    dims[dim] *= pieces.shape[0]
    return jnp.moveaxis(pieces, 0, dim).reshape(dims)


def copy_for_each(array, axis):
    length = lax.axis_size(axis)
    return lax.all_to_all(
        jnp.broadcast_to(array[None], (length, *array.shape)), axis, 0, 0, tiled=True
    )


def gathered_copies(array, axis, dim):
    return laid_out(copy_for_each(array, axis), dim)


def match_index(targets, slot_keys, slot_live):
    matches = (targets[..., None] == slot_keys) & slot_live
    ordinal = jnp.arange(1, slot_keys.shape[0] + 1, dtype=jnp.int32)
    located = jnp.sum(jnp.where(matches, ordinal, 0), axis=-1)
    return jnp.where(located > 0, located - 1, slot_keys.shape[0])


def local(x_blocks, x_slots, x_count, s_slots, s_count):
    row_total = lax.axis_size("row")
    col_total = lax.axis_size("col")
    row_id = lax.axis_index("row")
    col_id = lax.axis_index("col")
    capacity = x_blocks.shape[2]
    block_size = x_blocks.shape[3]
    order_blocks = RB * col_total
    tile_width = order_blocks // row_total
    panel_all = lax.all_gather(x_blocks, "row", axis=0, tiled=True)
    stacked = panel_all.reshape(row_total * capacity, block_size, block_size)
    padded = jnp.concatenate(
        [stacked, jnp.zeros((1, block_size, block_size), stacked.dtype)], axis=0
    )
    column_slots = lax.dynamic_index_in_dim(x_slots, col_id, 1, keepdims=False)
    column_count = lax.dynamic_index_in_dim(x_count, col_id, 1, keepdims=False)
    ordinal = jnp.arange(capacity, dtype=jnp.int32)
    panel_live = (ordinal[None, :] < column_count[:, None]).reshape(-1)
    owners = jnp.arange(row_total, dtype=jnp.int32)[:, None]
    panel_keys = (
        column_slots // tile_width * order_blocks + owners * tile_width + column_slots % tile_width
    ).reshape(-1)
    row_lanes = jnp.arange(RB, dtype=jnp.int32)
    window_ids = jnp.arange(JW, dtype=jnp.int32)

    def accumulate(running, values, inner_row, inner_col, usable):
        picked = match_index(
            row_lanes[None, :] * order_blocks + inner_row[:, None], panel_keys, panel_live
        )
        left_part = jnp.take(padded, picked, axis=0)
        placing = ((inner_col[:, None] == window_ids[None, :]) & usable[:, None]).astype(
            values.dtype
        )
        placed = placing[:, :, None, None] * values[:, None, :, :]
        return running + jnp.einsum(
            "nrxy,njyz->rjxz", left_part, placed, preferred_element_type=jnp.float32
        )

    def make_step(slot_table, count_row, stride, column_limit):

        def fold_step(running, piece, offset):
            pieces = piece.shape[1]
            slot_count = piece.shape[2]
            positions = lax.dynamic_slice_in_dim(slot_table, offset, pieces, 0)[:, :slot_count]
            counts = lax.dynamic_slice_in_dim(count_row, offset, pieces, 0)
            owner_ids = offset + jnp.arange(pieces, dtype=jnp.int32)[:, None]
            inner_row = owner_ids * RB + positions // stride
            inner_col = positions % stride
            usable = (jnp.arange(slot_count, dtype=jnp.int32)[None, :] < counts[:, None]) & (
                inner_col < column_limit
            )
            values = piece.reshape(pieces * slot_count, block_size, block_size)
            return accumulate(
                running, values, inner_row.reshape(-1), inner_col.reshape(-1), usable.reshape(-1)
            )

        return fold_step

    blank_sum = jnp.zeros((RB, JW, block_size, block_size), jnp.float32)

    def collect_all(gathered, fold_step):
        per_turn = math.gcd(col_total, 8)

        def advance(turn_index, running):
            offset = turn_index * per_turn
            portion = lax.dynamic_slice_in_dim(gathered, offset, per_turn, 1)
            return fold_step(running, portion, offset)

        return lax.fori_loop(0, col_total // per_turn, advance, blank_sum)

    row_slots = lax.dynamic_index_in_dim(x_slots, row_id, 0, keepdims=False)
    row_count = lax.dynamic_index_in_dim(x_count, row_id, 0, keepdims=False)
    square_slots = lax.dynamic_index_in_dim(s_slots, row_id, 0, keepdims=False)
    square_count = lax.dynamic_index_in_dim(s_count, row_id, 0, keepdims=False)
    window_part = x_blocks[:, :, :CAPW]
    first_step = make_step(row_slots, row_count, tile_width, JW)
    product = collect_all(gathered_copies(window_part, "col", 1), first_step)
    own_slots = lax.dynamic_index_in_dim(square_slots, col_id, 0, keepdims=False)
    own_count = lax.dynamic_index_in_dim(square_count, col_id, 0, keepdims=False)
    own_live = jnp.arange(own_slots.shape[0], dtype=jnp.int32) < own_count
    flat_one = product.reshape(RB * JW, block_size, block_size)
    square_part = jnp.where(
        own_live[:, None, None], jnp.take(flat_one, own_slots, axis=0), 0.0
    ).astype(jnp.bfloat16)
    square_part = square_part[None, None]
    second_step = make_step(square_slots, square_count, JW, JW)
    second = collect_all(gathered_copies(square_part, "col", 1), second_step)
    own_keys = own_slots // JW * order_blocks + row_id * tile_width + own_slots % JW
    own_block = jnp.take(padded, match_index(own_keys, panel_keys, panel_live), axis=0).astype(
        jnp.float32
    )
    flat_two = second.reshape(RB * JW, block_size, block_size)
    combined = 1.5 * own_block - 0.5 * jnp.take(flat_two, own_slots, axis=0)
    result = jnp.where(own_live[:, None, None], combined, 0.0).astype(jnp.bfloat16)
    return (square_part, result[None, None])


def solution(mesh):
    in_specs = (P("row", "col", None, None, None), P(), P(), P(), P())
    out_specs = (P("row", "col", None, None, None), P("row", "col", None, None, None))
    return jax.shard_map(local, mesh=mesh, in_specs=in_specs, out_specs=out_specs, check_vma=False)
```

profile of v0, /device:TPU:1, one launch (start us, length us, event | category | flops | bytes accessed | tf_op | source)
XLA Modules:
  0.0 268.8 jit_solution(12169378988364675214)
XLA Ops:
  7.9 0.8 slice_bitcast_fusion
  8.9 1.9 broadcast_in_dim.199
  10.8 11.9 %all-to-all-start = ((bf16[32,1,1,2,128,128]{4,5,3,2,1,0:T(8,128)(2,1)}), bf16[32,1,1,2,128,128]{4,5,3,2,1,0:T(8,128)(2,1)S(1)}, u32[]{:S(2)}, u32[]{:S(2)}) async-start(bf16[32,1,1,2,128,128]{4,5,3,2,1,0:T(8,128)(2,1)} %broadcast_in_dim.199), calls=%async_computation | async-start | bytes 4194304 | tf_op jit(solution)/shard_map/all_to_all | solution.py:20
  23.2 1.4 fusion.74
  25.5 1.3 dynamic_slice.97
  28.4 48.9 %all-gather.2.cloned.1.call-done = bf16[8,1,42,128,128]{4,3,2,1,0:T(8,128)(2,1)} async-done(((bf16[1,1,42,128,128]{4,3,2,1,0:T(8,128)(2,1)}), bf16[8,1,42,128,128]{4,3,2,1,0:T(8,128)(2,1)}) %all-gather.2.cloned.1.call-update) | async-done | bytes 11010064 | tf_op jit(solution)/shard_map/all_gather | solution.py:45
  77.3 10.6 %concatenate.3 = bf16[337,128,128]{2,1,0:T(8,128)(2,1)} pad(bf16[336,128,128]{2,1,0:T(8,128)(2,1)} %bitcast.101, bf16[]{:T(256)} %constant.410.clone.1), padding=0_1x0_0x0_0 | pad | bytes 22052866 | tf_op jit(solution)/shard_map/concatenate | solution.py:47
  87.9 54.0 %while.36 = (s32[]{:T(128)}, f32[8,2,128,128]{2,3,0,1:T(8,128)}, s32[32,42]{1,0:T(8,128)S(1)}, s32[32]{0:T(128)S(1)}, bf16[1,32,2,128,128]{3,4,2,1,0:T(8,128)(2,...) while((s32[]{:T(128)}, f32[8,2,128,128]{2,3,0,1:T(8,128)}, ...), condition=%wide.wide.region_2.4_spmd.clone, body=%wide.wide.region_0.3_spmd.clone.sunk | while | flops 1078636672 | bytes 16272037 | solution.py:104
  89.0 7.3 %gather_fusion = bf16[128,128,128]{2,1,0:T(8,128)(2,1)} fusion(bf16[337,128,128]{2,1,0:T(8,128)(2,1)} %get-tuple-element.924, s32[1024]{0:T(1024)S(1)} %pad_clamp_fusion.8), kind=kCustom, calls=%fused_computation.clone.clone.clone.1 | custom fusion | bytes 8389120 | tf_op jit(solution)/shard_map/while/body/eval_jaxpr/jit(_take)/gather | solution.py:65
  96.6 4.6 %fusion.100 = f32[8,2,128,128]{2,3,0,1:T(8,128)} fusion(bf16[16,8,128,128]{3,2,1,0:T(8,128)(2,1)} %bitcast.97, pred[16,8]{0,1:T(8,128)(4,1)S(1)} %copy.73, f32[8,2,128,128]{2,3,0,1:T(8,128)} %get-tuple-element.906, bf16[16,128,128]{1,2,0:T(8,128)(2,1)S(1)} %bitcast.99, bf16[16,2]{0,1:T(2,128)(2,1)S(1)} %and_convert_fusion.6, pred[]{:T(512)S(6)} %compare.58), kind=kOutput, calls=%fused_computation.17.clone.clone.1 | convolution fusion | flops 1078460416 | bytes 6815937 | tf_op jit(solution)/shard_map/while/body/eval_jaxpr/nrxy,njyz->rjxz/dot_general | solution.py:70
  102.3 7.3 %gather_fusion = bf16[128,128,128]{2,1,0:T(8,128)(2,1)} fusion(bf16[337,128,128]{2,1,0:T(8,128)(2,1)} %get-tuple-element.924, s32[1024]{0:T(1024)S(1)} %pad_clamp_fusion.8), kind=kCustom, calls=%fused_computation.clone.clone.clone.1 | custom fusion | bytes 8389120 | tf_op jit(solution)/shard_map/while/body/eval_jaxpr/jit(_take)/gather | solution.py:65
  109.9 4.8 %fusion.100 = f32[8,2,128,128]{2,3,0,1:T(8,128)} fusion(bf16[16,8,128,128]{3,2,1,0:T(8,128)(2,1)} %bitcast.97, pred[16,8]{0,1:T(8,128)(4,1)S(1)} %copy.73, f32[8,2,128,128]{2,3,0,1:T(8,128)} %get-tuple-element.906, bf16[16,128,128]{1,2,0:T(8,128)(2,1)S(1)} %bitcast.99, bf16[16,2]{0,1:T(2,128)(2,1)S(1)} %and_convert_fusion.6, pred[]{:T(512)S(6)} %compare.58), kind=kOutput, calls=%fused_computation.17.clone.clone.1 | convolution fusion | flops 1078460416 | bytes 6815937 | tf_op jit(solution)/shard_map/while/body/eval_jaxpr/nrxy,njyz->rjxz/dot_general | solution.py:70
  115.9 7.3 %gather_fusion = bf16[128,128,128]{2,1,0:T(8,128)(2,1)} fusion(bf16[337,128,128]{2,1,0:T(8,128)(2,1)} %get-tuple-element.924, s32[1024]{0:T(1024)S(1)} %pad_clamp_fusion.8), kind=kCustom, calls=%fused_computation.clone.clone.clone.1 | custom fusion | bytes 8389120 | tf_op jit(solution)/shard_map/while/body/eval_jaxpr/jit(_take)/gather | solution.py:65
  123.5 4.8 %fusion.100 = f32[8,2,128,128]{2,3,0,1:T(8,128)} fusion(bf16[16,8,128,128]{3,2,1,0:T(8,128)(2,1)} %bitcast.97, pred[16,8]{0,1:T(8,128)(4,1)S(1)} %copy.73, f32[8,2,128,128]{2,3,0,1:T(8,128)} %get-tuple-element.906, bf16[16,128,128]{1,2,0:T(8,128)(2,1)S(1)} %bitcast.99, bf16[16,2]{0,1:T(2,128)(2,1)S(1)} %and_convert_fusion.6, pred[]{:T(512)S(6)} %compare.58), kind=kOutput, calls=%fused_computation.17.clone.clone.1 | convolution fusion | flops 1078460416 | bytes 6815937 | tf_op jit(solution)/shard_map/while/body/eval_jaxpr/nrxy,njyz->rjxz/dot_general | solution.py:70
  129.4 7.3 %gather_fusion = bf16[128,128,128]{2,1,0:T(8,128)(2,1)} fusion(bf16[337,128,128]{2,1,0:T(8,128)(2,1)} %get-tuple-element.924, s32[1024]{0:T(1024)S(1)} %pad_clamp_fusion.8), kind=kCustom, calls=%fused_computation.clone.clone.clone.1 | custom fusion | bytes 8389120 | tf_op jit(solution)/shard_map/while/body/eval_jaxpr/jit(_take)/gather | solution.py:65
  137.0 4.8 %fusion.100 = f32[8,2,128,128]{2,3,0,1:T(8,128)} fusion(bf16[16,8,128,128]{3,2,1,0:T(8,128)(2,1)} %bitcast.97, pred[16,8]{0,1:T(8,128)(4,1)S(1)} %copy.73, f32[8,2,128,128]{2,3,0,1:T(8,128)} %get-tuple-element.906, bf16[16,128,128]{1,2,0:T(8,128)(2,1)S(1)} %bitcast.99, bf16[16,2]{0,1:T(2,128)(2,1)S(1)} %and_convert_fusion.6, pred[]{:T(512)S(6)} %compare.58), kind=kOutput, calls=%fused_computation.17.clone.clone.1 | convolution fusion | flops 1078460416 | bytes 6815937 | tf_op jit(solution)/shard_map/while/body/eval_jaxpr/nrxy,njyz->rjxz/dot_general | solution.py:70
  141.9 1.5 copy.37
  144.2 1.9 broadcast_in_dim.207
  146.0 9.6 %all-to-all-start.1 = ((bf16[32,1,1,2,128,128]{4,5,3,2,1,0:T(8,128)(2,1)}), bf16[32,1,1,2,128,128]{4,5,3,2,1,0:T(8,128)(2,1)S(1)}, u32[]{:S(2)}, u32[]{:S(2)}) async-start(bf16[32,1,1,2,128,128]{4,5,3,2,1,0:T(8,128)(2,1)} %broadcast_in_dim.207), calls=%async_computation.1 | async-start | bytes 4194304 | tf_op jit(solution)/shard_map/all_to_all | solution.py:20
  156.4 4.7 %gather_fusion.2 = bf16[2,128,128]{2,1,0:T(8,128)(2,1)S(1)} fusion(bf16[337,128,128]{2,1,0:T(8,128)(2,1)} %get-tuple-element.971, s32[1024]{0:T(1024)S(1)} %pad_clamp_fusion.2), kind=kCustom, calls=%fused_computation.4 | custom fusion | bytes 131080 | tf_op jit(solution)/shard_map/jit(_take)/gather | solution.py:124
  161.8 42.7 %all-to-all-done.1 = bf16[32,1,1,2,128,128]{4,5,3,2,1,0:T(8,128)(2,1)S(1)} async-done(((bf16[32,1,1,2,128,128]{4,5,3,2,1,0:T(8,128)(2,1)}), bf16[32,1,1,2,128,128]{4,5,3,2,1,0:T(8,128)(2,1)S(1)}, u32[]{:S(2)}, u32[]{:S(2)}) %all-to-all-start.1) | async-done | bytes 2097184 | tf_op jit(solution)/shard_map/all_to_all | solution.py:20
  204.5 54.6 %while.37 = (s32[]{:T(128)}, f32[8,2,128,128]{2,3,0,1:T(8,128)}, s32[32,2]{0,1:T(2,128)S(1)}, s32[32]{0:T(128)S(1)}, bf16[1,32,2,128,128]{3,4,2,1,0:T(8,128)(2,1...) while((s32[]{:T(128)}, f32[8,2,128,128]{2,3,0,1:T(8,128)}, ...), condition=%wide.wide.region_6.9_spmd.clone, body=%wide.wide.region_4.8_spmd.clone.sunk | while | flops 1078636672 | bytes 16269573 | solution.py:104
  206.0 7.3 %gather_fusion.1 = bf16[128,128,128]{2,1,0:T(8,128)(2,1)} fusion(bf16[337,128,128]{2,1,0:T(8,128)(2,1)} %get-tuple-element.963, s32[1024]{0:T(1024)S(1)} %pad_clamp_fusion.9), kind=kCustom, calls=%fused_computation.2.clone.clone.clone.1 | custom fusion | bytes 8389120 | tf_op jit(solution)/shard_map/while/body/eval_jaxpr/jit(_take)/gather | solution.py:65
  213.4 4.6 %fusion.105 = f32[8,2,128,128]{2,3,0,1:T(8,128)} fusion(bf16[16,8,128,128]{3,2,1,0:T(8,128)(2,1)} %bitcast.98, pred[16,8]{0,1:T(8,128)(4,1)S(1)} %copy.76, f32[8,2,128,128]{2,3,0,1:T(8,128)} %get-tuple-element.945, bf16[16,128,128]{1,2,0:T(8,128)(2,1)S(1)} %bitcast.100, bf16[16,2]{0,1:T(2,128)(2,1)S(1)} %and_convert_fusion.7, pred[]{:T(512)S(6)} %compare.59), kind=kOutput, calls=%fused_computation.53.clone.clone.1 | convolution fusion | flops 1078460416 | bytes 6815937 | tf_op jit(solution)/shard_map/while/body/eval_jaxpr/nrxy,njyz->rjxz/dot_general | solution.py:70
  219.4 7.3 %gather_fusion.1 = bf16[128,128,128]{2,1,0:T(8,128)(2,1)} fusion(bf16[337,128,128]{2,1,0:T(8,128)(2,1)} %get-tuple-element.963, s32[1024]{0:T(1024)S(1)} %pad_clamp_fusion.9), kind=kCustom, calls=%fused_computation.2.clone.clone.clone.1 | custom fusion | bytes 8389120 | tf_op jit(solution)/shard_map/while/body/eval_jaxpr/jit(_take)/gather | solution.py:65
  226.8 4.8 %fusion.105 = f32[8,2,128,128]{2,3,0,1:T(8,128)} fusion(bf16[16,8,128,128]{3,2,1,0:T(8,128)(2,1)} %bitcast.98, pred[16,8]{0,1:T(8,128)(4,1)S(1)} %copy.76, f32[8,2,128,128]{2,3,0,1:T(8,128)} %get-tuple-element.945, bf16[16,128,128]{1,2,0:T(8,128)(2,1)S(1)} %bitcast.100, bf16[16,2]{0,1:T(2,128)(2,1)S(1)} %and_convert_fusion.7, pred[]{:T(512)S(6)} %compare.59), kind=kOutput, calls=%fused_computation.53.clone.clone.1 | convolution fusion | flops 1078460416 | bytes 6815937 | tf_op jit(solution)/shard_map/while/body/eval_jaxpr/nrxy,njyz->rjxz/dot_general | solution.py:70
  233.1 7.3 %gather_fusion.1 = bf16[128,128,128]{2,1,0:T(8,128)(2,1)} fusion(bf16[337,128,128]{2,1,0:T(8,128)(2,1)} %get-tuple-element.963, s32[1024]{0:T(1024)S(1)} %pad_clamp_fusion.9), kind=kCustom, calls=%fused_computation.2.clone.clone.clone.1 | custom fusion | bytes 8389120 | tf_op jit(solution)/shard_map/while/body/eval_jaxpr/jit(_take)/gather | solution.py:65
  240.5 4.8 %fusion.105 = f32[8,2,128,128]{2,3,0,1:T(8,128)} fusion(bf16[16,8,128,128]{3,2,1,0:T(8,128)(2,1)} %bitcast.98, pred[16,8]{0,1:T(8,128)(4,1)S(1)} %copy.76, f32[8,2,128,128]{2,3,0,1:T(8,128)} %get-tuple-element.945, bf16[16,128,128]{1,2,0:T(8,128)(2,1)S(1)} %bitcast.100, bf16[16,2]{0,1:T(2,128)(2,1)S(1)} %and_convert_fusion.7, pred[]{:T(512)S(6)} %compare.59), kind=kOutput, calls=%fused_computation.53.clone.clone.1 | convolution fusion | flops 1078460416 | bytes 6815937 | tf_op jit(solution)/shard_map/while/body/eval_jaxpr/nrxy,njyz->rjxz/dot_general | solution.py:70
  246.8 7.3 %gather_fusion.1 = bf16[128,128,128]{2,1,0:T(8,128)(2,1)} fusion(bf16[337,128,128]{2,1,0:T(8,128)(2,1)} %get-tuple-element.963, s32[1024]{0:T(1024)S(1)} %pad_clamp_fusion.9), kind=kCustom, calls=%fused_computation.2.clone.clone.clone.1 | custom fusion | bytes 8389120 | tf_op jit(solution)/shard_map/while/body/eval_jaxpr/jit(_take)/gather | solution.py:65
  254.2 4.8 %fusion.105 = f32[8,2,128,128]{2,3,0,1:T(8,128)} fusion(bf16[16,8,128,128]{3,2,1,0:T(8,128)(2,1)} %bitcast.98, pred[16,8]{0,1:T(8,128)(4,1)S(1)} %copy.76, f32[8,2,128,128]{2,3,0,1:T(8,128)} %get-tuple-element.945, bf16[16,128,128]{1,2,0:T(8,128)(2,1)S(1)} %bitcast.100, bf16[16,2]{0,1:T(2,128)(2,1)S(1)} %and_convert_fusion.7, pred[]{:T(512)S(6)} %compare.59), kind=kOutput, calls=%fused_computation.53.clone.clone.1 | convolution fusion | flops 1078460416 | bytes 6815937 | tf_op jit(solution)/shard_map/while/body/eval_jaxpr/nrxy,njyz->rjxz/dot_general | solution.py:70
  259.1 1.6 copy.40
  261.2 0.7 fusion.54
  (216 shorter events, 18.4 us)
Async XLA Ops:
  7.2 18.2 %copy-start = (s32[8,32,2]{1,2,0:T(2,128)S(1)}, s32[8,32,2]{1,2,0:T(2,128)}, u32[]{:S(2)}) copy-start(s32[8,32,2]{1,2,0:T(2,128)} %param.16) | copy-start | bytes 6148
  7.2 17.6 %copy-start.3 = (s32[8,32]{1,0:T(8,128)S(1)}, s32[8,32]{1,0:T(8,128)}, u32[]{:S(2)}) copy-start(s32[8,32]{1,0:T(8,128)} %param.15) | copy-start | bytes 3076
  7.2 70.1 %all-gather.2.cloned.1.call-start = ((), (), s32[]{:S(2)}) async-start(), calls=%async_computation.2 | async-start | bytes 12386304 | tf_op jit(solution)/shard_map/all_gather | solution.py:45
  10.8 77.2 %all-to-all-start = ((bf16[32,1,1,2,128,128]{4,5,3,2,1,0:T(8,128)(2,1)}), bf16[32,1,1,2,128,128]{4,5,3,2,1,0:T(8,128)(2,1)S(1)}, u32[]{:S(2)}, u32[]{:S(2)}) async-start(bf16[32,1,1,2,128,128]{4,5,3,2,1,0:T(8,128)(2,1)} %broadcast_in_dim.199), calls=%async_computation | async-start | bytes 4194304 | tf_op jit(solution)/shard_map/all_to_all | solution.py:20
  24.7 63.2 %copy-start.1 = (s32[8,42]{1,0:T(8,128)}, s32[8,42]{1,0:T(8,128)S(1)}, u32[]{:S(2)}) copy-start(s32[8,42]{1,0:T(8,128)S(1)} %fusion.57) | copy-start | bytes 4036
  141.9 13.7 %copy-start.2 = (s32[8,42]{1,0:T(8,128)S(1)}, s32[8,42]{1,0:T(8,128)}, u32[]{:S(2)}) copy-start(s32[8,42]{1,0:T(8,128)} %get-tuple-element.981) | copy-start | bytes 4036
  146.0 58.5 %all-to-all-start.1 = ((bf16[32,1,1,2,128,128]{4,5,3,2,1,0:T(8,128)(2,1)}), bf16[32,1,1,2,128,128]{4,5,3,2,1,0:T(8,128)(2,1)S(1)}, u32[]{:S(2)}, u32[]{:S(2)}) async-start(bf16[32,1,1,2,128,128]{4,5,3,2,1,0:T(8,128)(2,1)} %broadcast_in_dim.207), calls=%async_computation.1 | async-start | bytes 4194304 | tf_op jit(solution)/shard_map/all_to_all | solution.py:20
Sparse Core Ops, SparseCore 0:
  9.8 67.4 all-gather.1
where the time goes:
time: 270 us; the launch traced here: 269 us
  local copies, waits for them, and re-layouts  93.6 us (35%)
  waiting for transfers between devices  92.3 us (34%)
  matrix products  38.2 us (14%)
  starting transfers between devices  21.5 us (8%)
  between operations  14.2 us (5%)
  other arithmetic  8.6 us (3%)
    gather x8, local copies, waits for them, and re-layouts, accumulate(): left_part = jnp.take(padded, picked, axis=0)  58.1 us
    all_gather x1, waiting for transfers between devices, local(): panel_all = lax.all_gather(x_blocks, 'row', axis=0, tiled=True)  48.9 us
    all_to_all x2, waiting for transfers between devices, copy_for_each(): lax.all_to_all(jnp.broadcast_to(array[None], (length, *array.shape)), axi...  42.7 us
    dot_general x8, matrix products, accumulate(): jnp.einsum('nrxy,njyz->rjxz', left_part, placed, preferred_element_type=j...  38.2 us
    all_to_all x2, starting transfers between devices, copy_for_each(): lax.all_to_all(jnp.broadcast_to(array[None], (length, *array.shape)), axi...  21.4 us
    concatenate x1, local copies, waits for them, and re-layouts, local(): jnp.concatenate([stacked, jnp.zeros((1, block_size, block_size), stacked....  10.6 us
  transfers between devices with their start and end apart: 3, of which 2 were waited for; matrix products, arithmetic and copies ran while one was open for 9% of the time, Pallas kernels for 0%

commit v1 on v0

--- a/solution.py
+++ b/solution.py
@@ -1,3 +1,4 @@
+import functools
 import math
 import jax
 import jax.numpy as jnp
@@ -7,6 +8,21 @@
 RB = 8
 JW = 2
 CAPW = 2
+
+
+def scan_lines(z, ax_name):
+    return jnp.concatenate(
+        lax.all_to_all(
+            jnp.stack([z] * lax.axis_size(ax_name), axis=0),
+            split_axis=0,
+            concat_axis=0,
+            axis_name=ax_name,
+        ),
+        axis=0,
+    )
+
+
+meet_circles = functools.partial(scan_lines, ax_name="row")
 
 
 def laid_out(pieces, dim):
@@ -42,7 +58,7 @@
     block_size = x_blocks.shape[3]
     order_blocks = RB * col_total
     tile_width = order_blocks // row_total
-    panel_all = lax.all_gather(x_blocks, "row", axis=0, tiled=True)
+    panel_all = meet_circles(x_blocks)
     stacked = panel_all.reshape(row_total * capacity, block_size, block_size)
     padded = jnp.concatenate(
         [stacked, jnp.zeros((1, block_size, block_size), stacked.dtype)], axis=0

time: 270 us -> 372 us (1.38)
  waiting for transfers between devices: 92.3 us -> 195 us
  between operations: 14.2 us -> 0.79 us
  local copies, waits for them, and re-layouts: 93.6 us -> 102 us
    all_to_all x0 -> x1, waiting for transfers between devices: none -> 121 us  [scan_lines(): lax.all_to_all(jnp.stack([z] * lax.axis_size(ax_name), axis=0), split_axi...]
    all_gather x1 -> x0, waiting for transfers between devices: 48.9 us -> none  [local(): panel_all = lax.all_gather(x_blocks, 'row', axis=0, tiled=True)]
    all_to_all x2, waiting for transfers between devices: 42.7 us -> 74.6 us  [copy_for_each(): lax.all_to_all(jnp.broadcast_to(array[None], (length, *array.shape)), axi...]
    another operation x0 -> x1, local copies, waits for them, and re-layouts: none -> 8.33 us  [scan_lines(): jnp.stack([z] * lax.axis_size(ax_name), axis=0)]
    all_to_all x0 -> x1, starting transfers between devices: none -> 8.26 us  [scan_lines(): lax.all_to_all(jnp.stack([z] * lax.axis_size(ax_name), axis=0), split_axi...]
    all_to_all x2, starting transfers between devices: 21.4 us -> 16.4 us  [copy_for_each(): lax.all_to_all(jnp.broadcast_to(array[None], (length, *array.shape)), axi...]
  transfers between devices with their start and end apart: 3 -> 3, of which waited for: 2 -> 3; matrix products, arithmetic and copies ran while one was open for 9% -> 6% of each run, Pallas kernels for 0% -> 0%
where the time goes in v1:
time: 372 us; the launch traced here: 370 us
  waiting for transfers between devices  195 us (52%)
  local copies, waits for them, and re-layouts  102 us (27%)
  matrix products  38.2 us (10%)
  starting transfers between devices  24.7 us (7%)
  other arithmetic  8.73 us (2%)
    all_to_all x1, waiting for transfers between devices, scan_lines(): lax.all_to_all(jnp.stack([z] * lax.axis_size(ax_name), axis=0), split_axi...  121 us
    all_to_all x2, waiting for transfers between devices, copy_for_each(): lax.all_to_all(jnp.broadcast_to(array[None], (length, *array.shape)), axi...  74.6 us
    gather x8, local copies, waits for them, and re-layouts, accumulate(): left_part = jnp.take(padded, picked, axis=0)  58 us
    dot_general x8, matrix products, accumulate(): jnp.einsum('nrxy,njyz->rjxz', left_part, placed, preferred_element_type=j...  38.2 us
    all_to_all x2, starting transfers between devices, copy_for_each(): lax.all_to_all(jnp.broadcast_to(array[None], (length, *array.shape)), axi...  16.4 us
    concatenate x1, local copies, waits for them, and re-layouts, local(): jnp.concatenate([stacked, jnp.zeros((1, block_size, block_size), stacked....  10.6 us
    another operation x1, local copies, waits for them, and re-layouts, scan_lines(): jnp.stack([z] * lax.axis_size(ax_name), axis=0)  8.33 us
    all_to_all x1, starting transfers between devices, scan_lines(): lax.all_to_all(jnp.stack([z] * lax.axis_size(ax_name), axis=0), split_axi...  8.26 us
  transfers between devices with their start and end apart: 3, of which 3 were waited for; matrix products, arithmetic and copies ran while one was open for 6% of the time, Pallas kernels for 0%

profile of v1, /device:TPU:1, one launch (start us, length us, event | category | flops | bytes accessed | tf_op | source)
XLA Modules:
  0.0 370.3 jit_solution(8045077735970027891)
XLA Ops:
  0.6 8.3 %stack.2 = bf16[8,1,1,42,128,128]{5,4,3,2,1,0:T(8,128)(2,1)} broadcast(bf16[42,128,128]{2,1,0:T(8,128)(2,1)} %bitcast.104), dimensions={3,4,5} | broadcast | bytes 12386304 | tf_op jit(solution)/shard_map/stack | solution.py:16
  9.0 8.3 %all-to-all-start.1 = ((bf16[8,1,1,42,128,128]{5,4,3,2,1,0:T(8,128)(2,1)}), bf16[8,1,1,42,128,128]{5,4,3,2,1,0:T(8,128)(2,1)}, u32[]{:S(2)}, u32[]{:S(2)}) async-start(bf16[8,1,1,42,128,128]{5,4,3,2,1,0:T(8,128)(2,1)} %stack.2), calls=%async_computation.1 | async-start | bytes 22020096 | tf_op jit(solution)/shard_map/all_to_all | solution.py:15
  18.2 120.9 %all-to-all-done.1 = bf16[8,1,1,42,128,128]{5,4,3,2,1,0:T(8,128)(2,1)} async-done(((bf16[8,1,1,42,128,128]{5,4,3,2,1,0:T(8,128)(2,1)}), bf16[8,1,1,42,128,128]{5,4,3,2,1,0:T(8,128)(2,1)}, u32[]{:S(2)}, u32[]{:S(2)}) %all-to-all-start.1) | async-done | bytes 11010080 | tf_op jit(solution)/shard_map/all_to_all | solution.py:15
  139.1 1.9 broadcast_in_dim.199
  140.9 9.3 %all-to-all-start = ((bf16[32,1,1,2,128,128]{4,5,3,2,1,0:T(8,128)(2,1)}), bf16[32,1,1,2,128,128]{4,5,3,2,1,0:T(8,128)(2,1)S(1)}, u32[]{:S(2)}, u32[]{:S(2)}) async-start(bf16[32,1,1,2,128,128]{4,5,3,2,1,0:T(8,128)(2,1)} %broadcast_in_dim.199), calls=%async_computation | async-start | bytes 4194304 | tf_op jit(solution)/shard_map/all_to_all | solution.py:36
  150.8 1.4 fusion.74
  156.2 10.6 %concatenate.3 = bf16[337,128,128]{2,1,0:T(8,128)(2,1)} pad(bf16[336,128,128]{2,1,0:T(8,128)(2,1)} %bitcast.7, bf16[]{:T(256)} %constant.410.clone.1), padding=0_1x0_0x0_0 | pad | bytes 22052866 | tf_op jit(solution)/shard_map/concatenate | solution.py:63
  166.8 32.1 %all-to-all-done = bf16[32,1,1,2,128,128]{4,5,3,2,1,0:T(8,128)(2,1)S(1)} async-done(((bf16[32,1,1,2,128,128]{4,5,3,2,1,0:T(8,128)(2,1)}), bf16[32,1,1,2,128,128]{4,5,3,2,1,0:T(8,128)(2,1)S(1)}, u32[]{:S(2)}, u32[]{:S(2)}) %all-to-all-start) | async-done | bytes 2097184 | tf_op jit(solution)/shard_map/all_to_all | solution.py:36
  199.0 53.9 %while.36 = (s32[]{:T(128)}, f32[8,2,128,128]{2,3,0,1:T(8,128)}, s32[32,42]{1,0:T(8,128)S(1)}, s32[32]{0:T(128)S(1)}, bf16[1,32,2,128,128]{3,4,2,1,0:T(8,128)(2,...) while((s32[]{:T(128)}, f32[8,2,128,128]{2,3,0,1:T(8,128)}, ...), condition=%wide.wide.region_2.4_spmd.clone, body=%wide.wide.region_0.3_spmd.clone.sunk | while | flops 1078636672 | bytes 16272037 | solution.py:120
  200.1 7.3 %gather_fusion = bf16[128,128,128]{2,1,0:T(8,128)(2,1)} fusion(bf16[337,128,128]{2,1,0:T(8,128)(2,1)} %get-tuple-element.924, s32[1024]{0:T(1024)S(1)} %pad_clamp_fusion.8), kind=kCustom, calls=%fused_computation.clone.clone.clone.1 | custom fusion | bytes 8389120 | tf_op jit(solution)/shard_map/while/body/eval_jaxpr/jit(_take)/gather | solution.py:81
  207.7 4.6 %fusion.100 = f32[8,2,128,128]{2,3,0,1:T(8,128)} fusion(bf16[16,8,128,128]{3,2,1,0:T(8,128)(2,1)} %bitcast.98, pred[16,8]{0,1:T(8,128)(4,1)S(1)} %copy.73, f32[8,2,128,128]{2,3,0,1:T(8,128)} %get-tuple-element.906, bf16[16,128,128]{1,2,0:T(8,128)(2,1)S(1)} %bitcast.100, bf16[16,2]{0,1:T(2,128)(2,1)S(1)} %and_convert_fusion.6, pred[]{:T(512)S(6)} %compare.58), kind=kOutput, calls=%fused_computation.17.clone.clone.1 | convolution fusion | flops 1078460416 | bytes 6815937 | tf_op jit(solution)/shard_map/while/body/eval_jaxpr/nrxy,njyz->rjxz/dot_general | solution.py:86
  213.3 7.3 %gather_fusion = bf16[128,128,128]{2,1,0:T(8,128)(2,1)} fusion(bf16[337,128,128]{2,1,0:T(8,128)(2,1)} %get-tuple-element.924, s32[1024]{0:T(1024)S(1)} %pad_clamp_fusion.8), kind=kCustom, calls=%fused_computation.clone.clone.clone.1 | custom fusion | bytes 8389120 | tf_op jit(solution)/shard_map/while/body/eval_jaxpr/jit(_take)/gather | solution.py:81
  220.9 4.8 %fusion.100 = f32[8,2,128,128]{2,3,0,1:T(8,128)} fusion(bf16[16,8,128,128]{3,2,1,0:T(8,128)(2,1)} %bitcast.98, pred[16,8]{0,1:T(8,128)(4,1)S(1)} %copy.73, f32[8,2,128,128]{2,3,0,1:T(8,128)} %get-tuple-element.906, bf16[16,128,128]{1,2,0:T(8,128)(2,1)S(1)} %bitcast.100, bf16[16,2]{0,1:T(2,128)(2,1)S(1)} %and_convert_fusion.6, pred[]{:T(512)S(6)} %compare.58), kind=kOutput, calls=%fused_computation.17.clone.clone.1 | convolution fusion | flops 1078460416 | bytes 6815937 | tf_op jit(solution)/shard_map/while/body/eval_jaxpr/nrxy,njyz->rjxz/dot_general | solution.py:86
  226.9 7.3 %gather_fusion = bf16[128,128,128]{2,1,0:T(8,128)(2,1)} fusion(bf16[337,128,128]{2,1,0:T(8,128)(2,1)} %get-tuple-element.924, s32[1024]{0:T(1024)S(1)} %pad_clamp_fusion.8), kind=kCustom, calls=%fused_computation.clone.clone.clone.1 | custom fusion | bytes 8389120 | tf_op jit(solution)/shard_map/while/body/eval_jaxpr/jit(_take)/gather | solution.py:81
  234.5 4.8 %fusion.100 = f32[8,2,128,128]{2,3,0,1:T(8,128)} fusion(bf16[16,8,128,128]{3,2,1,0:T(8,128)(2,1)} %bitcast.98, pred[16,8]{0,1:T(8,128)(4,1)S(1)} %copy.73, f32[8,2,128,128]{2,3,0,1:T(8,128)} %get-tuple-element.906, bf16[16,128,128]{1,2,0:T(8,128)(2,1)S(1)} %bitcast.100, bf16[16,2]{0,1:T(2,128)(2,1)S(1)} %and_convert_fusion.6, pred[]{:T(512)S(6)} %compare.58), kind=kOutput, calls=%fused_computation.17.clone.clone.1 | convolution fusion | flops 1078460416 | bytes 6815937 | tf_op jit(solution)/shard_map/while/body/eval_jaxpr/nrxy,njyz->rjxz/dot_general | solution.py:86
  240.4 7.3 %gather_fusion = bf16[128,128,128]{2,1,0:T(8,128)(2,1)} fusion(bf16[337,128,128]{2,1,0:T(8,128)(2,1)} %get-tuple-element.924, s32[1024]{0:T(1024)S(1)} %pad_clamp_fusion.8), kind=kCustom, calls=%fused_computation.clone.clone.clone.1 | custom fusion | bytes 8389120 | tf_op jit(solution)/shard_map/while/body/eval_jaxpr/jit(_take)/gather | solution.py:81
  248.0 4.8 %fusion.100 = f32[8,2,128,128]{2,3,0,1:T(8,128)} fusion(bf16[16,8,128,128]{3,2,1,0:T(8,128)(2,1)} %bitcast.98, pred[16,8]{0,1:T(8,128)(4,1)S(1)} %copy.73, f32[8,2,128,128]{2,3,0,1:T(8,128)} %get-tuple-element.906, bf16[16,128,128]{1,2,0:T(8,128)(2,1)S(1)} %bitcast.100, bf16[16,2]{0,1:T(2,128)(2,1)S(1)} %and_convert_fusion.6, pred[]{:T(512)S(6)} %compare.58), kind=kOutput, calls=%fused_computation.17.clone.clone.1 | convolution fusion | flops 1078460416 | bytes 6815937 | tf_op jit(solution)/shard_map/while/body/eval_jaxpr/nrxy,njyz->rjxz/dot_general | solution.py:86
  252.8 1.5 copy.37
  255.1 1.9 broadcast_in_dim.207
  257.0 7.1 %all-to-all-start.2 = ((bf16[32,1,1,2,128,128]{4,5,3,2,1,0:T(8,128)(2,1)}), bf16[32,1,1,2,128,128]{4,5,3,2,1,0:T(8,128)(2,1)S(1)}, u32[]{:S(2)}, u32[]{:S(2)}) async-start(bf16[32,1,1,2,128,128]{4,5,3,2,1,0:T(8,128)(2,1)} %broadcast_in_dim.207), calls=%async_computation.2 | async-start | bytes 4194304 | tf_op jit(solution)/shard_map/all_to_all | solution.py:36
  264.9 4.7 %gather_fusion.2 = bf16[2,128,128]{2,1,0:T(8,128)(2,1)S(1)} fusion(bf16[337,128,128]{2,1,0:T(8,128)(2,1)} %get-tuple-element.970, s32[1024]{0:T(1024)S(1)} %pad_clamp_fusion.2), kind=kCustom, calls=%fused_computation.4 | custom fusion | bytes 131080 | tf_op jit(solution)/shard_map/jit(_take)/gather | solution.py:140
  270.4 42.5 %all-to-all-done.2 = bf16[32,1,1,2,128,128]{4,5,3,2,1,0:T(8,128)(2,1)S(1)} async-done(((bf16[32,1,1,2,128,128]{4,5,3,2,1,0:T(8,128)(2,1)}), bf16[32,1,1,2,128,128]{4,5,3,2,1,0:T(8,128)(2,1)S(1)}, u32[]{:S(2)}, u32[]{:S(2)}) %all-to-all-start.2) | async-done | bytes 2097184 | tf_op jit(solution)/shard_map/all_to_all | solution.py:36
  312.8 54.6 %while.37 = (s32[]{:T(128)}, f32[8,2,128,128]{2,3,0,1:T(8,128)}, s32[32,2]{0,1:T(2,128)S(1)}, s32[32]{0:T(128)S(1)}, bf16[1,32,2,128,128]{3,4,2,1,0:T(8,128)(2,1...) while((s32[]{:T(128)}, f32[8,2,128,128]{2,3,0,1:T(8,128)}, ...), condition=%wide.wide.region_6.9_spmd.clone, body=%wide.wide.region_4.8_spmd.clone.sunk | while | flops 1078636672 | bytes 16269573 | solution.py:120
  314.3 7.3 %gather_fusion.1 = bf16[128,128,128]{2,1,0:T(8,128)(2,1)} fusion(bf16[337,128,128]{2,1,0:T(8,128)(2,1)} %get-tuple-element.963, s32[1024]{0:T(1024)S(1)} %pad_clamp_fusion.9), kind=kCustom, calls=%fused_computation.2.clone.clone.clone.1 | custom fusion | bytes 8389120 | tf_op jit(solution)/shard_map/while/body/eval_jaxpr/jit(_take)/gather | solution.py:81
  321.7 4.6 %fusion.105 = f32[8,2,128,128]{2,3,0,1:T(8,128)} fusion(bf16[16,8,128,128]{3,2,1,0:T(8,128)(2,1)} %bitcast.99, pred[16,8]{0,1:T(8,128)(4,1)S(1)} %copy.76, f32[8,2,128,128]{2,3,0,1:T(8,128)} %get-tuple-element.945, bf16[16,128,128]{1,2,0:T(8,128)(2,1)S(1)} %bitcast.101, bf16[16,2]{0,1:T(2,128)(2,1)S(1)} %and_convert_fusion.7, pred[]{:T(512)S(6)} %compare.59), kind=kOutput, calls=%fused_computation.53.clone.clone.1 | convolution fusion | flops 1078460416 | bytes 6815937 | tf_op jit(solution)/shard_map/while/body/eval_jaxpr/nrxy,njyz->rjxz/dot_general | solution.py:86
  327.7 7.3 %gather_fusion.1 = bf16[128,128,128]{2,1,0:T(8,128)(2,1)} fusion(bf16[337,128,128]{2,1,0:T(8,128)(2,1)} %get-tuple-element.963, s32[1024]{0:T(1024)S(1)} %pad_clamp_fusion.9), kind=kCustom, calls=%fused_computation.2.clone.clone.clone.1 | custom fusion | bytes 8389120 | tf_op jit(solution)/shard_map/while/body/eval_jaxpr/jit(_take)/gather | solution.py:81
  335.1 4.9 %fusion.105 = f32[8,2,128,128]{2,3,0,1:T(8,128)} fusion(bf16[16,8,128,128]{3,2,1,0:T(8,128)(2,1)} %bitcast.99, pred[16,8]{0,1:T(8,128)(4,1)S(1)} %copy.76, f32[8,2,128,128]{2,3,0,1:T(8,128)} %get-tuple-element.945, bf16[16,128,128]{1,2,0:T(8,128)(2,1)S(1)} %bitcast.101, bf16[16,2]{0,1:T(2,128)(2,1)S(1)} %and_convert_fusion.7, pred[]{:T(512)S(6)} %compare.59), kind=kOutput, calls=%fused_computation.53.clone.clone.1 | convolution fusion | flops 1078460416 | bytes 6815937 | tf_op jit(solution)/shard_map/while/body/eval_jaxpr/nrxy,njyz->rjxz/dot_general | solution.py:86
  341.4 7.3 %gather_fusion.1 = bf16[128,128,128]{2,1,0:T(8,128)(2,1)} fusion(bf16[337,128,128]{2,1,0:T(8,128)(2,1)} %get-tuple-element.963, s32[1024]{0:T(1024)S(1)} %pad_clamp_fusion.9), kind=kCustom, calls=%fused_computation.2.clone.clone.clone.1 | custom fusion | bytes 8389120 | tf_op jit(solution)/shard_map/while/body/eval_jaxpr/jit(_take)/gather | solution.py:81
  348.8 4.9 %fusion.105 = f32[8,2,128,128]{2,3,0,1:T(8,128)} fusion(bf16[16,8,128,128]{3,2,1,0:T(8,128)(2,1)} %bitcast.99, pred[16,8]{0,1:T(8,128)(4,1)S(1)} %copy.76, f32[8,2,128,128]{2,3,0,1:T(8,128)} %get-tuple-element.945, bf16[16,128,128]{1,2,0:T(8,128)(2,1)S(1)} %bitcast.101, bf16[16,2]{0,1:T(2,128)(2,1)S(1)} %and_convert_fusion.7, pred[]{:T(512)S(6)} %compare.59), kind=kOutput, calls=%fused_computation.53.clone.clone.1 | convolution fusion | flops 1078460416 | bytes 6815937 | tf_op jit(solution)/shard_map/while/body/eval_jaxpr/nrxy,njyz->rjxz/dot_general | solution.py:86
  355.1 7.3 %gather_fusion.1 = bf16[128,128,128]{2,1,0:T(8,128)(2,1)} fusion(bf16[337,128,128]{2,1,0:T(8,128)(2,1)} %get-tuple-element.963, s32[1024]{0:T(1024)S(1)} %pad_clamp_fusion.9), kind=kCustom, calls=%fused_computation.2.clone.clone.clone.1 | custom fusion | bytes 8389120 | tf_op jit(solution)/shard_map/while/body/eval_jaxpr/jit(_take)/gather | solution.py:81
  362.5 4.9 %fusion.105 = f32[8,2,128,128]{2,3,0,1:T(8,128)} fusion(bf16[16,8,128,128]{3,2,1,0:T(8,128)(2,1)} %bitcast.99, pred[16,8]{0,1:T(8,128)(4,1)S(1)} %copy.76, f32[8,2,128,128]{2,3,0,1:T(8,128)} %get-tuple-element.945, bf16[16,128,128]{1,2,0:T(8,128)(2,1)S(1)} %bitcast.101, bf16[16,2]{0,1:T(2,128)(2,1)S(1)} %and_convert_fusion.7, pred[]{:T(512)S(6)} %compare.59), kind=kOutput, calls=%fused_computation.53.clone.clone.1 | convolution fusion | flops 1078460416 | bytes 6815937 | tf_op jit(solution)/shard_map/while/body/eval_jaxpr/nrxy,njyz->rjxz/dot_general | solution.py:86
  367.4 1.6 copy.40
  (216 shorter events, 20.7 us)
Async XLA Ops:
  0.6 152.4 %copy-start = (s32[8,32,2]{1,2,0:T(2,128)S(1)}, s32[8,32,2]{1,2,0:T(2,128)}, u32[]{:S(2)}) copy-start(s32[8,32,2]{1,2,0:T(2,128)} %param.16) | copy-start | bytes 6148
  9.0 130.1 %all-to-all-start.1 = ((bf16[8,1,1,42,128,128]{5,4,3,2,1,0:T(8,128)(2,1)}), bf16[8,1,1,42,128,128]{5,4,3,2,1,0:T(8,128)(2,1)}, u32[]{:S(2)}, u32[]{:S(2)}) async-start(bf16[8,1,1,42,128,128]{5,4,3,2,1,0:T(8,128)(2,1)} %stack.2), calls=%async_computation.1 | async-start | bytes 22020096 | tf_op jit(solution)/shard_map/all_to_all | solution.py:15
  17.2 135.2 %copy-start.3 = (s32[8,32]{1,0:T(8,128)S(1)}, s32[8,32]{1,0:T(8,128)}, u32[]{:S(2)}) copy-start(s32[8,32]{1,0:T(8,128)} %param.15) | copy-start | bytes 3076
  140.9 58.0 %all-to-all-start = ((bf16[32,1,1,2,128,128]{4,5,3,2,1,0:T(8,128)(2,1)}), bf16[32,1,1,2,128,128]{4,5,3,2,1,0:T(8,128)(2,1)S(1)}, u32[]{:S(2)}, u32[]{:S(2)}) async-start(bf16[32,1,1,2,128,128]{4,5,3,2,1,0:T(8,128)(2,1)} %broadcast_in_dim.199), calls=%async_computation | async-start | bytes 4194304 | tf_op jit(solution)/shard_map/all_to_all | solution.py:36
  152.3 14.5 %copy-start.1 = (s32[8,42]{1,0:T(8,128)}, s32[8,42]{1,0:T(8,128)S(1)}, u32[]{:S(2)}) copy-start(s32[8,42]{1,0:T(8,128)S(1)} %fusion.57) | copy-start | bytes 4036
  252.8 11.3 %copy-start.2 = (s32[8,42]{1,0:T(8,128)S(1)}, s32[8,42]{1,0:T(8,128)}, u32[]{:S(2)}) copy-start(s32[8,42]{1,0:T(8,128)} %get-tuple-element.979) | copy-start | bytes 4036
  257.0 55.8 %all-to-all-start.2 = ((bf16[32,1,1,2,128,128]{4,5,3,2,1,0:T(8,128)(2,1)}), bf16[32,1,1,2,128,128]{4,5,3,2,1,0:T(8,128)(2,1)S(1)}, u32[]{:S(2)}, u32[]{:S(2)}) async-start(bf16[32,1,1,2,128,128]{4,5,3,2,1,0:T(8,128)(2,1)} %broadcast_in_dim.207), calls=%async_computation.2 | async-start | bytes 4194304 | tf_op jit(solution)/shard_map/all_to_all | solution.py:36
